TPU v7x, 32 devices: a whole 2x2x4 slice. The times are simulated.
32 devices in a mesh: dp: 8 (over z, x), expert: 4 (over y, core).
Axes of the slice: x: 2, y: 2, z: 4, core: 2. Of those that a mesh axis runs over, the one named last changes fastest.
Arguments:
- out_grad: bfloat16 [8192, 1024], P(('dp', 'expert')), may hold values from -6 to 6
- expert_of: int32 [8192, 1], P(('dp', 'expert')), may hold values from 0 to 3; in each aligned block of 256 rows (0 to 255, 256 to 511, ...) at most 128 rows name the same one
- pre_act: bfloat16 [16384, 4096], P(('dp', 'expert')), may hold values from -6 to 6
- down_weight: bfloat16 [4, 4096, 1024], P('expert', 'dp'), may hold values from -0.09375 to 0.09375
Outputs:
- pre_grad: bfloat16 [16384, 4096], P(('dp', 'expert'))
- weight_grad: float32 [4, 4096, 1024], P('expert', 'dp')
Inputs may be any that keep to these rules, and one draw needn't show every extreme that they name: `expert_of`: within each aligned block of 256 rows (the rows of one device) no expert is named by more than 128 rows, and in some blocks one expert is named by exactly 128 rows.
All inputs are finite; a program needn't handle non-finite values.
Results may differ from a plain program's by a relative error of at most 0.0026.
Values may be sent and summed in bfloat16 or wider, within the bound.
A program may use at most 128 MiB of HBM per device.

v0:
```python
import math

import jax
import jax.numpy as jnp
from jax import lax
from jax.sharding import PartitionSpec as P

tanh_scale = 0.7978845608028654
cubic_weight = 0.044715


def activate(values):
    argument = tanh_scale * (values + cubic_weight * values * values * values)
    return 0.5 * values * (1.0 + jnp.tanh(argument))


def derivative(values):
    tangent = jnp.tanh(tanh_scale * (values + cubic_weight * values * values * values))
    return 0.5 * (1.0 + tangent) + 0.5 * values * (1.0 - tangent * tangent) * tanh_scale * (
        1.0 + 3.0 * cubic_weight * values * values
    )


def body(out_grad, expert_of, pre_act, down_weight):
    experts = lax.axis_size("expert")
    replicas = lax.axis_size("dp")
    token_count = out_grad.shape[0]
    model_width = out_grad.shape[1]
    capacity = token_count // 2
    routed = expert_of[:, 0]
    onehot = (routed[:, None] == jnp.arange(experts, dtype=jnp.int32)[None, :]).astype(jnp.int32)
    position = jnp.sum((jnp.cumsum(onehot, axis=0) - onehot) * onehot, axis=1)
    target = routed * capacity + position
    outgoing = jnp.zeros((experts * capacity, model_width), jnp.bfloat16).at[target].set(out_grad)
    arrived = lax.all_to_all(
        outgoing.reshape(experts, capacity, model_width),
        "expert",
        split_axis=0,
        concat_axis=0,
        tiled=True,
    )
    arrived = arrived.reshape(experts * capacity, model_width)
    weight = down_weight[0]
    own_rows = weight.shape[0]
    factor = 1.0 / math.sqrt(replicas * token_count)
    hidden_grad = lax.dot_general(
        arrived,
        lax.all_gather(weight, "dp", axis=0, tiled=True),
        (((1,), (1,)), ((), ())),
        preferred_element_type=jnp.float32,
    )
    pre_block = pre_act.astype(jnp.float32)
    pre_grad = (hidden_grad * derivative(pre_block)).astype(jnp.bfloat16)
    pre_block = pre_act.astype(jnp.float32)
    hidden = activate(pre_block).astype(jnp.bfloat16)
    summed = lax.psum_scatter(
        lax.dot_general(
            hidden, arrived, (((0,), (0,)), ((), ())), preferred_element_type=jnp.float32
        ),
        "dp",
        scatter_dimension=0,
        tiled=True,
    )
    return (pre_grad, (summed * factor).reshape(1, own_rows, model_width))


def solution(mesh):
    placed = (
        P(("dp", "expert"), None),
        P(("dp", "expert"), None),
        P(("dp", "expert"), None),
        P("expert", "dp", None),
    )
    return jax.shard_map(
        body,
        mesh=mesh,
        in_specs=placed,
        out_specs=(P(("dp", "expert"), None), P("expert", "dp", None)),
        check_vma=False,
    )
```

profile of v0, /device:TPU:0, one launch (start us, length us, event | category | flops | bytes accessed | tf_op | source)
XLA Modules:
  0.0 429.0 jit_solution(12696060192646106825)
XLA Ops:
  7.2 0.0 all-gather.3.cloned.1.call-start
  7.2 0.7 all-gather.3.cloned.1.call-update
  7.9 0.0 reduce-scatter.2.cloned.1.call-start
  7.9 0.7 compare_convert_fusion
  8.6 1.2 reduce-window.6
  9.8 0.1 slice.8
  9.9 0.1 copy.8
  10.1 0.1 copy.9
  10.2 0.1 add_bitcast_fusion
  10.2 0.7 fusion.25
  10.9 0.7 compare_select_fusion
  11.6 2.4 scatter_custom_fusion
  14.0 18.5 %all_to_all.5 = bf16[4,128,1024]{2,1,0:T(8,128)(2,1)S(1)} all-to-all(bf16[4,128,1024]{2,1,0:T(8,128)(2,1)S(1)} %bitcast.34), channel_id=1, replica_groups=mesh['dp'=8,'expert'=4] {'expert'}, dimensions={0} | all-to-all | bytes 2097152 | tf_op jit(solution)/shard_map/all_to_all | solution.py:35
  32.5 14.0 %fusion.13 = f32[4096,1024]{1,0:T(8,128)} fusion(bf16[512,1024]{1,0:T(8,128)(2,1)S(1)} %bitcast.35, bf16[512,4096]{1,0:T(8,128)(2,1)} %param.6), kind=kOutput, calls=%fused_computation.21 | convolution fusion | flops 4315938816 | bytes 22020096 | tf_op jit(solution)/shard_map/dot_general | solution.py:57
  46.6 0.0 reduce-scatter.2.cloned.1.call-update
  46.6 90.7 %all-gather.3.cloned.1.call-done = bf16[1,4096,1024]{2,1,0:T(8,128)(2,1)} async-done(((bf16[1,512,1024]{2,1,0:T(8,128)(2,1)}), bf16[1,4096,1024]{2,1,0:T(8,128)(2,1)}) %all-gather.3.cloned.1.call-update) | async-done | bytes 8388624 | tf_op jit(solution)/shard_map/all_gather | solution.py:48
  137.3 14.3 %fusion.6 = bf16[512,4096]{1,0:T(8,128)(2,1)} fusion(bf16[512,4096]{1,0:T(8,128)(2,1)} %param.6, bf16[512,1024]{1,0:T(8,128)(2,1)S(1)} %bitcast.36, bf16[1,4096,1024]{2,1,0:T(8,128)(2,1)} %all-gather.3.cloned.1.call-done), kind=kOutput, calls=%fused_computation.14 | convolution fusion | flops 4336910336 | bytes 17825792 | tf_op jit(solution)/shard_map/dot_general | solution.py:46
  151.6 267.2 %reduce-scatter.2.cloned.1.call-done = f32[512,1024]{1,0:T(8,128)} async-done(((f32[4096,1024]{1,0:T(8,128)}), f32[512,1024]{1,0:T(8,128)}) %reduce-scatter.2.cloned.1.call-update) | async-done | bytes 2097168 | tf_op jit(solution)/shard_map/reduce_scatter | solution.py:56
  418.9 3.3 multiply_bitcast_fusion
  (2 shorter events, 0.0 us)
Async XLA Ops:
  7.2 130.2 %all-gather.3.cloned.1.call-start = ((), (), s32[]{:S(2)}) async-start(), calls=%async_computation.3 | async-start | bytes 9437184 | tf_op jit(solution)/shard_map/all_gather | solution.py:48
  7.9 411.0 %reduce-scatter.2.cloned.1.call-start = ((), (), s32[]{:S(2)}) async-start(), calls=%async_computation.2 | async-start | bytes 18874368 | tf_op jit(solution)/shard_map/reduce_scatter | solution.py:56
Sparse Core Ops, SparseCore 0:
  10.1 127.1 all-gather.2
  141.1 277.7 reduce-scatter.1
where the time goes:
time: 429 us
  waiting for transfers between devices  359 us (84%)
  matrix products  28.3 us (7%)
  blocking collectives  18.5 us (4%)
  between operations  14 us (3%)
  other arithmetic  6.68 us (2%)
    reduce_scatter x1, waiting for transfers between devices, body(): lax.psum_scatter(lax.dot_general(hidden, arrived, (((0,), (0,)), ((), ())...  267 us
    all_gather x1, waiting for transfers between devices, body(): lax.all_gather(weight, 'dp', axis=0, tiled=True)  90.7 us
    all_to_all x1, blocking collectives, body(): lax.all_to_all(outgoing.reshape(experts, capacity, model_width), 'expert'...  18.5 us
    dot_general x1, matrix products, body(): lax.dot_general(arrived, lax.all_gather(weight, 'dp', axis=0, tiled=True)...  14.3 us
    dot_general x1, matrix products, body(): lax.dot_general(hidden, arrived, (((0,), (0,)), ((), ())), preferred_elem...  14 us
  transfers between devices with their start and end apart: 2, of which 2 were waited for; matrix products, arithmetic and copies ran while one was open for 8% of the time, Pallas kernels for 0%

commit v1 on v0

--- a/solution.py
+++ b/solution.py
@@ -1,12 +1,19 @@
+import functools
 import math
 
 import jax
 import jax.numpy as jnp
 from jax import lax
+from jax.experimental import pallas as pl
+from jax.experimental.pallas import tpu as pltpu
 from jax.sharding import PartitionSpec as P
 
 tanh_scale = 0.7978845608028654
 cubic_weight = 0.044715
+MESH = pl.DeviceIdType.MESH
+PAIR = 2
+LINE = 4
+CUTS = 2
 
 
 def activate(values):
@@ -21,9 +28,432 @@
     )
 
 
+def kernel(
+    experts,
+    capacity,
+    factor,
+    tokens_ref,
+    route_ref,
+    pre_hbm,
+    weight_hbm,
+    grad_hbm,
+    dw_ref,
+    their_tokens,
+    their_route,
+    outgoing,
+    arrived,
+    pre_own,
+    pre_theirs,
+    weights,
+    hidden,
+    slope,
+    partial,
+    sums_out,
+    sums_in,
+    grad_own,
+    grad_theirs,
+    token_sems,
+    send_sems,
+    arrive_sems,
+    local_sems,
+    pre_sems,
+    weight_send,
+    weight_recv,
+    sum_send,
+    sum_recv,
+    grad_sems,
+):
+    d = lax.axis_index("dp")
+    me = lax.axis_index("expert")
+    z = lax.div(d, PAIR)
+    x = lax.rem(d, PAIR)
+    partner = z * PAIR + 1 - x
+    rows, width = pre_hbm.shape[0], tokens_ref.shape[1]
+    block = weight_hbm.shape[0]
+    count = tokens_ref.shape[0]
+    low = z < LINE // 2
+
+    def order(i):
+        if i == LINE - 1:
+            return z
+        down = LINE - 1 - i
+        return jnp.where(
+            low, jnp.where(down > z, down, down - 1), jnp.where(i < z, i, i + 1)
+        )
+
+    def columns(j, side):
+        return pl.ds(pl.multiple_of((j * PAIR + side) * block, block), block)
+
+    barrier = pltpu.get_barrier_semaphore()
+    pl.semaphore_signal(barrier, inc=1, device_id={"dp": partner}, device_id_type=MESH)
+    for k in range(1, experts):
+        pl.semaphore_signal(
+            barrier, inc=1, device_id={"expert": lax.rem(me + k, experts)}, device_id_type=MESH
+        )
+
+    @pl.when(z > 0)
+    def _():
+        pl.semaphore_signal(barrier, inc=1, device_id={"dp": d - PAIR}, device_id_type=MESH)
+
+    @pl.when(z < LINE - 1)
+    def _():
+        pl.semaphore_signal(barrier, inc=1, device_id={"dp": d + PAIR}, device_id_type=MESH)
+
+    inner = jnp.where((z > 0) & (z < LINE - 1), 2, 1)
+    pl.semaphore_wait(barrier, experts + inner)
+
+    def remote(src, dst, send, recv, device):
+        return pltpu.make_async_remote_copy(
+            src_ref=src, dst_ref=dst, send_sem=send, recv_sem=recv,
+            device_id=device, device_id_type=MESH,
+        )
+
+    route_copy = remote(
+        route_ref, their_route, token_sems.at[0], token_sems.at[1], {"dp": partner}
+    )
+    token_copy = remote(
+        tokens_ref, their_tokens, token_sems.at[2], token_sems.at[3], {"dp": partner}
+    )
+    route_copy.start()
+    token_copy.start()
+
+    def weight_copy(direction, hop):
+        step = 1 - 2 * direction
+        shard = z - step * hop
+        shard = jnp.clip(shard, 0, LINE - 1)
+        src = weight_hbm if hop == 0 else weights.at[shard]
+        return remote(
+            src, weights.at[shard], weight_send.at[direction, hop],
+            weight_recv.at[direction, hop], {"dp": d + step * PAIR},
+        )
+
+    def sends(direction, hop):
+        if direction == 0:
+            return (z >= hop) & (z < LINE - 1)
+        return (z <= LINE - 1 - hop) & (z > 0)
+
+    def receives(direction, hop):
+        return (z > hop) if direction == 0 else (z < LINE - 1 - hop)
+
+    def weight_start(hop):
+        for direction in range(2):
+            @pl.when(sends(direction, hop))
+            def _():
+                weight_copy(direction, hop).start()
+
+    def weight_arrive(hop):
+        for direction in range(2):
+            @pl.when(receives(direction, hop))
+            def _():
+                step = 1 - 2 * direction
+                shard = jnp.clip(z - step * (hop + 1), 0, LINE - 1)
+                remote(
+                    weight_hbm, weights.at[shard], weight_send.at[direction, hop],
+                    weight_recv.at[direction, hop], {"dp": partner},
+                ).wait_recv()
+
+    weight_start(0)
+
+    def pre_copy(i):
+        return remote(
+            pre_hbm.at[:, columns(order(i), 1 - x)], pre_theirs.at[i],
+            pre_sems.at[0, i], pre_sems.at[1, i], {"dp": partner},
+        )
+
+    for i in range(LINE):
+        pre_copy(i).start()
+
+    def own_copy(i):
+        return pltpu.make_async_copy(
+            pre_hbm.at[:, columns(order(i), x)], pre_own.at[i], local_sems.at[i]
+        )
+
+    for i in range(LINE):
+        own_copy(i).start()
+    weight_own = pltpu.make_async_copy(weight_hbm, weights.at[z], local_sems.at[LINE])
+    weight_own.start()
+
+    def slots(source):
+        return pl.ds(pl.multiple_of(source * capacity, capacity), capacity)
+
+    def arrival(rep, k):
+        source = lax.rem(me + experts - k, experts)
+        return remote(
+            outgoing.at[rep, k - 1],
+            arrived.at[rep, slots(source)],
+            send_sems.at[rep, k - 1],
+            arrive_sems.at[rep, k - 1],
+            {"expert": lax.rem(me + k, experts)},
+        )
+
+    earlier = (
+        lax.broadcasted_iota(jnp.int32, (count, count), 0)
+        < lax.broadcasted_iota(jnp.int32, (count, count), 1)
+    ).astype(jnp.float32).astype(jnp.bfloat16)
+
+    def dispatch(rep, routes, tokens):
+        names = routes[...]
+        named = lax.broadcasted_iota(jnp.int32, (8, count), 0) == names
+        onehot = named.astype(jnp.float32)
+        before = jnp.dot(
+            onehot.astype(jnp.bfloat16), earlier, preferred_element_type=jnp.float32
+        )
+        position = jnp.sum(onehot * before, axis=0, keepdims=True).astype(jnp.int32)
+        slot = lax.broadcasted_iota(jnp.int32, (capacity, count), 0)
+        for k in list(range(1, experts)) + [0]:
+            target = lax.rem(me + k, experts)
+            place = jnp.where(names == target, position, -1)
+            choose = (slot == place).astype(jnp.float32).astype(jnp.bfloat16)
+            rows_out = jnp.dot(
+                choose, tokens[...], preferred_element_type=jnp.float32
+            ).astype(jnp.bfloat16)
+            if k == 0:
+                arrived[rep, slots(me), :] = rows_out
+            else:
+                outgoing[rep, k - 1] = rows_out
+                remote(
+                    outgoing.at[rep, k - 1],
+                    arrived.at[rep, slots(me)],
+                    send_sems.at[rep, k - 1],
+                    arrive_sems.at[rep, k - 1],
+                    {"expert": target},
+                ).start()
+
+    dispatch(0, route_ref, tokens_ref)
+
+    strip = 64
+
+    def activate_rows(rep, i, source):
+        @pl.loop(0, rows // (2 * strip))
+        def _(t):
+            for half in range(2):
+                at = pl.ds(pl.multiple_of(t * 2 * strip + half * strip, strip), strip)
+                v = source[i, at, :].astype(jnp.float32)
+                square = v * v
+                tangent = jnp.tanh(tanh_scale * v * (1.0 + cubic_weight * square))
+                gate = 0.5 * (1.0 + tangent)
+                slope[rep, i, at, :] = gate + 0.5 * v * (1.0 - tangent * tangent) * tanh_scale * (
+                    1.0 + 3.0 * cubic_weight * square
+                )
+                hidden[rep, i, at, :] = (v * gate).astype(jnp.bfloat16)
+
+    route_copy.wait_recv()
+    token_copy.wait_recv()
+    dispatch(1, their_route, their_tokens)
+    for i in range(LINE):
+        own_copy(i).wait()
+        activate_rows(0, i, pre_own)
+
+    weight_arrive(0)
+    weight_start(1)
+    for rep in range(2):
+        for k in range(1, experts):
+            arrival(rep, k).wait_recv()
+
+    tile = 256
+
+    def multiply(i):
+        pre_copy(i).wait_recv()
+        activate_rows(1, i, pre_theirs)
+
+        @pl.loop(0, block // tile)
+        def _(t):
+            at = pl.ds(pl.multiple_of(t * tile, tile), tile)
+            total = lax.dot_general(
+                hidden[0, i, :, at], arrived[0], (((0,), (0,)), ((), ())),
+                preferred_element_type=jnp.float32,
+            )
+            partial[i, at, :] = total + lax.dot_general(
+                hidden[1, i, :, at], arrived[1], (((0,), (0,)), ((), ())),
+                preferred_element_type=jnp.float32,
+            )
+
+    piece = block // CUTS
+
+    def sum_copy(direction, stage, cut):
+        part = pl.ds(cut * piece, piece)
+        return remote(
+            sums_out.at[direction, stage, part], sums_in.at[direction, stage, part],
+            sum_send.at[direction, stage, cut], sum_recv.at[direction, stage, cut],
+            {"dp": d + (1 - 2 * direction) * PAIR},
+        )
+
+    def pass_on(i, ends):
+        j = order(i)
+        for direction in range(2):
+            distance = (j - z) if direction == 0 else (z - j)
+            first = (z == 0) if direction == 0 else (z == LINE - 1)
+            stage = jnp.clip(LINE - 1 - distance, 0, LINE - 2)
+            if ends:
+                @pl.when((distance > 0) & first)
+                def _():
+                    for cut in range(CUTS):
+                        part = pl.ds(cut * piece, piece)
+                        sums_out[direction, stage, part, :] = partial[i, part, :].astype(
+                            jnp.bfloat16
+                        )
+                        sum_copy(direction, stage, cut).start()
+            else:
+                @pl.when((distance > 0) & jnp.logical_not(first))
+                def _():
+                    last = jnp.clip(stage - 1, 0, LINE - 2)
+                    for cut in range(CUTS):
+                        part = pl.ds(cut * piece, piece)
+                        sum_copy(direction, last, cut).wait_recv()
+                        sums_out[direction, stage, part, :] = (
+                            partial[i, part, :]
+                            + sums_in[direction, last, part, :].astype(jnp.float32)
+                        ).astype(jnp.bfloat16)
+                        sum_copy(direction, stage, cut).start()
+
+    def grad_copy(i):
+        return remote(
+            grad_theirs.at[i], grad_hbm.at[:, columns(order(i), x)],
+            grad_sems.at[0, i], grad_sems.at[1, i], {"dp": partner},
+        )
+
+    def grad_arrive(i):
+        return remote(
+            grad_theirs.at[i], grad_hbm.at[:, columns(order(i), 1 - x)],
+            grad_sems.at[0, i], grad_sems.at[1, i], {"dp": partner},
+        )
+
+    def grad_write(i):
+        return pltpu.make_async_copy(
+            grad_own.at[i], grad_hbm.at[:, columns(order(i), x)], grad_sems.at[2, i]
+        )
+
+    def differentiate(i):
+        j = order(i)
+        for rep, result in ((1, grad_theirs), (0, grad_own)):
+            @pl.loop(0, rows // tile)
+            def _(t):
+                at = pl.ds(pl.multiple_of(t * tile, tile), tile)
+                product = lax.dot_general(
+                    arrived[rep, at, :], weights[j], (((1,), (1,)), ((), ())),
+                    preferred_element_type=jnp.float32,
+                )
+                result[i, at, :] = (product * slope[rep, i, at, :]).astype(jnp.bfloat16)
+
+            if rep == 1:
+                grad_copy(i).start()
+            else:
+                grad_write(i).start()
+
+    multiply(0)
+    pass_on(0, True)
+    multiply(1)
+    pass_on(1, True)
+    weight_arrive(1)
+    weight_start(2)
+    weight_own.wait()
+    pass_on(0, False)
+    multiply(2)
+    pass_on(2, True)
+    differentiate(2)
+    differentiate(1)
+    multiply(3)
+    differentiate(3)
+    weight_arrive(2)
+    differentiate(0)
+    pass_on(1, False)
+    pass_on(2, False)
+
+    for cut in range(CUTS):
+        part = pl.ds(cut * piece, piece)
+        dw_ref[part, :] = partial[LINE - 1, part, :]
+        for direction in range(2):
+            @pl.when(receives(direction, 0))
+            def _():
+                sum_copy(direction, LINE - 2, cut).wait_recv()
+                dw_ref[part, :] += sums_in[direction, LINE - 2, part, :].astype(jnp.float32)
+        dw_ref[part, :] = dw_ref[part, :] * factor
+
+    for i in range(LINE):
+        grad_arrive(i).wait_recv()
+        grad_write(i).wait()
+    route_copy.wait_send()
+    token_copy.wait_send()
+    for i in range(LINE):
+        pre_copy(i).wait_send()
+        grad_copy(i).wait_send()
+    for rep in range(2):
+        for k in range(1, experts):
+            arrival(rep, k).wait_send()
+    for hop in range(LINE - 1):
+        for direction in range(2):
+            @pl.when(sends(direction, hop))
+            def _():
+                weight_copy(direction, hop).wait_send()
+    for stage in range(LINE - 1):
+        for direction in range(2):
+            toward = (z <= stage) if direction == 0 else (z >= LINE - 1 - stage)
+            inside = (z < LINE - 1) if direction == 0 else (z > 0)
+
+            @pl.when(toward & inside)
+            def _():
+                for cut in range(CUTS):
+                    sum_copy(direction, stage, cut).wait_send()
+
+
+def fused(out_grad, expert_of, pre_act, down_weight):
+    experts = lax.axis_size("expert")
+    replicas = lax.axis_size("dp")
+    count, width = out_grad.shape
+    rows, units = pre_act.shape
+    block = down_weight.shape[1]
+    capacity = count // 2
+    factor = 1.0 / math.sqrt(replicas * count)
+    half, full = jnp.bfloat16, jnp.float32
+    vmem = pl.BlockSpec(memory_space=pltpu.VMEM)
+    anywhere = pl.BlockSpec(memory_space=pl.ANY)
+    dma = pltpu.SemaphoreType.DMA
+    pre_grad, summed = pl.pallas_call(
+        functools.partial(kernel, experts, capacity, factor),
+        out_shape=(
+            jax.ShapeDtypeStruct((rows, units), half),
+            jax.ShapeDtypeStruct((block, width), full),
+        ),
+        in_specs=[vmem, vmem, anywhere, anywhere],
+        out_specs=(anywhere, vmem),
+        scratch_shapes=[
+            pltpu.VMEM((count, width), half),
+            pltpu.VMEM((1, count), jnp.int32),
+            pltpu.VMEM((2, experts - 1, capacity, width), half),
+            pltpu.VMEM((2, rows, width), half),
+            pltpu.VMEM((LINE, rows, block), half),
+            pltpu.VMEM((LINE, rows, block), half),
+            pltpu.VMEM((LINE, block, width), half),
+            pltpu.VMEM((2, LINE, rows, block), half),
+            pltpu.VMEM((2, LINE, rows, block), full),
+            pltpu.VMEM((LINE, block, width), full),
+            pltpu.VMEM((2, LINE - 1, block, width), half),
+            pltpu.VMEM((2, LINE - 1, block, width), half),
+            pltpu.VMEM((LINE, rows, block), half),
+            pltpu.VMEM((LINE, rows, block), half),
+            dma((4,)),
+            dma((2, experts - 1)),
+            dma((2, experts - 1)),
+            dma((LINE + 1,)),
+            dma((2, LINE)),
+            dma((2, LINE - 1)),
+            dma((2, LINE - 1)),
+            dma((2, LINE - 1, CUTS)),
+            dma((2, LINE - 1, CUTS)),
+            dma((3, LINE)),
+        ],
+        compiler_params=pltpu.CompilerParams(
+            collective_id=0, has_side_effects=True, vmem_limit_bytes=60 * 1024 * 1024
+        ),
+    )(out_grad, expert_of.reshape(1, count), pre_act, down_weight[0])
+    return pre_grad, summed.reshape(1, block, width)
+
+
 def body(out_grad, expert_of, pre_act, down_weight):
     experts = lax.axis_size("expert")
     replicas = lax.axis_size("dp")
+    if replicas == PAIR * LINE and experts <= 8:
+        return fused(out_grad, expert_of, pre_act, down_weight)
     token_count = out_grad.shape[0]
     model_width = out_grad.shape[1]
     capacity = token_count // 2
@@ -51,7 +481,6 @@
     )
     pre_block = pre_act.astype(jnp.float32)
     pre_grad = (hidden_grad * derivative(pre_block)).astype(jnp.bfloat16)
-    pre_block = pre_act.astype(jnp.float32)
     hidden = activate(pre_block).astype(jnp.bfloat16)
     summed = lax.psum_scatter(
         lax.dot_general(

time: 429 us -> 117 us (0.27)
  waiting for transfers between devices: 359 us -> 0 us
  Pallas kernels: 0 us -> 110 us
  matrix products: 28.3 us -> 0 us
  blocking collectives: 18.5 us -> 0 us
  between operations: 14 us -> 0.65 us
  other arithmetic: 6.68 us -> 0 us
    reduce_scatter x1 -> x0, waiting for transfers between devices: 267 us -> none  [body(): lax.psum_scatter(lax.dot_general(hidden, arrived, (((0,), (0,)), ((), ())...]
    pallas_call x0 -> x1, Pallas kernels: none -> 110 us  [fused(): pl.pallas_call(functools.partial(kernel, experts, capacity, factor), out_...]
    all_gather x1 -> x0, waiting for transfers between devices: 90.7 us -> none  [body(): lax.all_gather(weight, 'dp', axis=0, tiled=True)]
    dot_general x2 -> x0, matrix products: 28.3 us -> none  [the longest x1 14.3 us: body(): lax.dot_general(arrived, lax.all_gather(weight, 'dp', axis=0, tiled=True)...]
    all_to_all x1 -> x0, blocking collectives: 18.5 us -> none  [body(): lax.all_to_all(outgoing.reshape(experts, capacity, model_width), 'expert'...]
    unnamed x0 -> x4, local copies, waits for them, and re-layouts: none -> 6.17 us
  transfers between devices with their start and end apart: 2 -> 0, of which waited for: 2 -> 0; matrix products, arithmetic and copies ran while one was open for 8% -> 0% of each run, Pallas kernels for 0% -> 0%
where the time goes in v1:
time: 117 us
  Pallas kernels  110 us (94%)
  local copies, waits for them, and re-layouts  6.17 us (5%)
    pallas_call x1, Pallas kernels, fused(): pl.pallas_call(functools.partial(kernel, experts, capacity, factor), out_...  110 us
    unnamed x4, local copies, waits for them, and re-layouts  6.17 us

profile of v1, /device:TPU:0, one launch (start us, length us, event | category | flops | bytes accessed | tf_op | source)
XLA Modules:
  0.0 116.6 jit_solution(9662430419090102624)
XLA Ops:
  0.6 109.8 %shard_map.59 = (bf16[512,4096]{1,0:T(8,128)(2,1)}, f32[512,1024]{1,0:T(8,128)}) custom-call(bf16[256,1024]{1,0:T(8,128)(2,1)} %tokens_ref.1, s32[1,256]{1,0:T(1,128)} %bitcast.5, bf16[512,4096]{1,0:T(8,128)(2,1)} %pre_hbm.1, bf16[512,1024]{1,0:T(8,128)(2,1)} %bitcast.4), custom_call_target="tpu_custom_call" | custom-call | tf_op jit(solution)/shard_map/pallas_call | solution.py:411
  110.5 0.0 copy-start
  110.5 4.8 %copy.8 = bf16[512,4096]{1,0:T(8,128)(2,1)} copy(bf16[512,4096]{1,0:T(8,128)(2,1)} %get-tuple-element.8) | data formatting | bytes 8388608
  115.3 0.0 copy-done
  115.3 1.3 %copy.9 = f32[1,512,1024]{2,1,0:T(8,128)} copy(f32[1,512,1024]{2,1,0:T(8,128)S(1)} %bitcast.3) | data formatting | bytes 4194304
Async XLA Ops:
  110.5 4.9 %copy-start = (f32[512,1024]{1,0:T(8,128)S(1)}, f32[512,1024]{1,0:T(8,128)}, u32[]{:S(2)}) copy-start(f32[512,1024]{1,0:T(8,128)} %get-tuple-element.5) | copy-start | bytes 6291460

commit v2 on v1

--- a/solution.py
+++ b/solution.py
@@ -37,7 +37,7 @@
     pre_hbm,
     weight_hbm,
     grad_hbm,
-    dw_ref,
+    dw_hbm,
     their_tokens,
     their_route,
     outgoing,
@@ -50,8 +50,6 @@
     partial,
     sums_out,
     sums_in,
-    grad_own,
-    grad_theirs,
     token_sems,
     send_sems,
     arrive_sems,
@@ -81,8 +79,13 @@
             low, jnp.where(down > z, down, down - 1), jnp.where(i < z, i, i + 1)
         )
 
+    piece = block // CUTS
+
     def columns(j, side):
         return pl.ds(pl.multiple_of((j * PAIR + side) * block, block), block)
+
+    def within(cut):
+        return pl.ds(pl.multiple_of(cut * piece, piece), piece)
 
     barrier = pltpu.get_barrier_semaphore()
     pl.semaphore_signal(barrier, inc=1, device_id={"dp": partner}, device_id_type=MESH)
@@ -154,14 +157,17 @@
 
     weight_start(0)
 
-    def pre_copy(i):
+    def pre_copy(i, cut):
+        start = (order(i) * PAIR + 1 - x) * block + cut * piece
         return remote(
-            pre_hbm.at[:, columns(order(i), 1 - x)], pre_theirs.at[i],
-            pre_sems.at[0, i], pre_sems.at[1, i], {"dp": partner},
+            pre_hbm.at[:, pl.ds(pl.multiple_of(start, piece), piece)],
+            pre_theirs.at[i, :, within(cut)],
+            pre_sems.at[0, i, cut], pre_sems.at[1, i, cut], {"dp": partner},
         )
 
     for i in range(LINE):
-        pre_copy(i).start()
+        for cut in range(CUTS):
+            pre_copy(i, cut).start()
 
     def own_copy(i):
         return pltpu.make_async_copy(
@@ -223,26 +229,31 @@
 
     strip = 64
 
-    def activate_rows(rep, i, source):
+    def activate_rows(rep, i, source, cut):
+        at_columns = within(cut)
+
         @pl.loop(0, rows // (2 * strip))
         def _(t):
             for half in range(2):
                 at = pl.ds(pl.multiple_of(t * 2 * strip + half * strip, strip), strip)
-                v = source[i, at, :].astype(jnp.float32)
+                v = source[i, at, at_columns].astype(jnp.float32)
                 square = v * v
                 tangent = jnp.tanh(tanh_scale * v * (1.0 + cubic_weight * square))
                 gate = 0.5 * (1.0 + tangent)
-                slope[rep, i, at, :] = gate + 0.5 * v * (1.0 - tangent * tangent) * tanh_scale * (
-                    1.0 + 3.0 * cubic_weight * square
-                )
-                hidden[rep, i, at, :] = (v * gate).astype(jnp.bfloat16)
+                slope[rep, i, at, at_columns] = gate + 0.5 * v * (
+                    1.0 - tangent * tangent
+                ) * tanh_scale * (1.0 + 3.0 * cubic_weight * square)
+                hidden[rep, i, at, at_columns] = (v * gate).astype(jnp.bfloat16)
 
     route_copy.wait_recv()
     token_copy.wait_recv()
     dispatch(1, their_route, their_tokens)
     for i in range(LINE):
         own_copy(i).wait()
-        activate_rows(0, i, pre_own)
+
+        @pl.loop(0, CUTS)
+        def _(cut):
+            activate_rows(0, i, pre_own, cut)
 
     weight_arrive(0)
     weight_start(1)
@@ -253,12 +264,11 @@
     tile = 256
 
     def multiply(i):
-        pre_copy(i).wait_recv()
-        activate_rows(1, i, pre_theirs)
-
-        @pl.loop(0, block // tile)
-        def _(t):
-            at = pl.ds(pl.multiple_of(t * tile, tile), tile)
+        @pl.loop(0, CUTS)
+        def _(cut):
+            pre_copy(i, cut).wait_recv()
+            activate_rows(1, i, pre_theirs, cut)
+            at = within(cut)
             total = lax.dot_general(
                 hidden[0, i, :, at], arrived[0], (((0,), (0,)), ((), ())),
                 preferred_element_type=jnp.float32,
@@ -267,19 +277,20 @@
                 hidden[1, i, :, at], arrived[1], (((0,), (0,)), ((), ())),
                 preferred_element_type=jnp.float32,
             )
-
-    piece = block // CUTS
+            if i < LINE - 1:
+                pass_on(i, True, cut)
 
     def sum_copy(direction, stage, cut):
-        part = pl.ds(cut * piece, piece)
+        part = within(cut)
         return remote(
             sums_out.at[direction, stage, part], sums_in.at[direction, stage, part],
             sum_send.at[direction, stage, cut], sum_recv.at[direction, stage, cut],
             {"dp": d + (1 - 2 * direction) * PAIR},
         )
 
-    def pass_on(i, ends):
+    def pass_on(i, ends, cut):
         j = order(i)
+        part = within(cut)
         for direction in range(2):
             distance = (j - z) if direction == 0 else (z - j)
             first = (z == 0) if direction == 0 else (z == LINE - 1)
@@ -287,45 +298,47 @@
             if ends:
                 @pl.when((distance > 0) & first)
                 def _():
-                    for cut in range(CUTS):
-                        part = pl.ds(cut * piece, piece)
-                        sums_out[direction, stage, part, :] = partial[i, part, :].astype(
-                            jnp.bfloat16
-                        )
-                        sum_copy(direction, stage, cut).start()
+                    sums_out[direction, stage, part, :] = partial[i, part, :].astype(
+                        jnp.bfloat16
+                    )
+                    sum_copy(direction, stage, cut).start()
             else:
                 @pl.when((distance > 0) & jnp.logical_not(first))
                 def _():
                     last = jnp.clip(stage - 1, 0, LINE - 2)
-                    for cut in range(CUTS):
-                        part = pl.ds(cut * piece, piece)
-                        sum_copy(direction, last, cut).wait_recv()
-                        sums_out[direction, stage, part, :] = (
-                            partial[i, part, :]
-                            + sums_in[direction, last, part, :].astype(jnp.float32)
-                        ).astype(jnp.bfloat16)
-                        sum_copy(direction, stage, cut).start()
+                    sum_copy(direction, last, cut).wait_recv()
+                    sums_out[direction, stage, part, :] = (
+                        partial[i, part, :]
+                        + sums_in[direction, last, part, :].astype(jnp.float32)
+                    ).astype(jnp.bfloat16)
+                    sum_copy(direction, stage, cut).start()
+
+    def forward(*blocks):
+        @pl.loop(0, CUTS)
+        def _(cut):
+            for i in blocks:
+                pass_on(i, False, cut)
 
     def grad_copy(i):
         return remote(
-            grad_theirs.at[i], grad_hbm.at[:, columns(order(i), x)],
+            pre_theirs.at[i], grad_hbm.at[:, columns(order(i), x)],
             grad_sems.at[0, i], grad_sems.at[1, i], {"dp": partner},
         )
 
     def grad_arrive(i):
         return remote(
-            grad_theirs.at[i], grad_hbm.at[:, columns(order(i), 1 - x)],
+            pre_theirs.at[i], grad_hbm.at[:, columns(order(i), 1 - x)],
             grad_sems.at[0, i], grad_sems.at[1, i], {"dp": partner},
         )
 
     def grad_write(i):
         return pltpu.make_async_copy(
-            grad_own.at[i], grad_hbm.at[:, columns(order(i), x)], grad_sems.at[2, i]
+            pre_own.at[i], grad_hbm.at[:, columns(order(i), x)], grad_sems.at[2, i]
         )
 
     def differentiate(i):
         j = order(i)
-        for rep, result in ((1, grad_theirs), (0, grad_own)):
+        for rep, result in ((1, pre_theirs), (0, pre_own)):
             @pl.loop(0, rows // tile)
             def _(t):
                 at = pl.ds(pl.multiple_of(t * tile, tile), tile)
@@ -341,41 +354,46 @@
                 grad_write(i).start()
 
     multiply(0)
-    pass_on(0, True)
     multiply(1)
-    pass_on(1, True)
     weight_arrive(1)
     weight_start(2)
     weight_own.wait()
-    pass_on(0, False)
+    forward(0)
     multiply(2)
-    pass_on(2, True)
     differentiate(2)
     differentiate(1)
     multiply(3)
     differentiate(3)
     weight_arrive(2)
     differentiate(0)
-    pass_on(1, False)
-    pass_on(2, False)
+    forward(1, 2)
+
+    def result_copy(cut):
+        part = pl.ds(cut * piece, piece)
+        return pltpu.make_async_copy(
+            partial.at[LINE - 1, part], dw_hbm.at[part], local_sems.at[LINE + 1 + cut]
+        )
 
     for cut in range(CUTS):
         part = pl.ds(cut * piece, piece)
-        dw_ref[part, :] = partial[LINE - 1, part, :]
         for direction in range(2):
             @pl.when(receives(direction, 0))
             def _():
                 sum_copy(direction, LINE - 2, cut).wait_recv()
-                dw_ref[part, :] += sums_in[direction, LINE - 2, part, :].astype(jnp.float32)
-        dw_ref[part, :] = dw_ref[part, :] * factor
+                partial[LINE - 1, part, :] += sums_in[direction, LINE - 2, part, :].astype(jnp.float32)
+        partial[LINE - 1, part, :] = partial[LINE - 1, part, :] * factor
+        result_copy(cut).start()
 
     for i in range(LINE):
         grad_arrive(i).wait_recv()
         grad_write(i).wait()
+    for cut in range(CUTS):
+        result_copy(cut).wait()
     route_copy.wait_send()
     token_copy.wait_send()
     for i in range(LINE):
-        pre_copy(i).wait_send()
+        for cut in range(CUTS):
+            pre_copy(i, cut).wait_send()
         grad_copy(i).wait_send()
     for rep in range(2):
         for k in range(1, experts):
@@ -415,7 +433,7 @@
             jax.ShapeDtypeStruct((block, width), full),
         ),
         in_specs=[vmem, vmem, anywhere, anywhere],
-        out_specs=(anywhere, vmem),
+        out_specs=(anywhere, anywhere),
         scratch_shapes=[
             pltpu.VMEM((count, width), half),
             pltpu.VMEM((1, count), jnp.int32),
@@ -429,13 +447,11 @@
             pltpu.VMEM((LINE, block, width), full),
             pltpu.VMEM((2, LINE - 1, block, width), half),
             pltpu.VMEM((2, LINE - 1, block, width), half),
-            pltpu.VMEM((LINE, rows, block), half),
-            pltpu.VMEM((LINE, rows, block), half),
             dma((4,)),
             dma((2, experts - 1)),
             dma((2, experts - 1)),
-            dma((LINE + 1,)),
-            dma((2, LINE)),
+            dma((LINE + 1 + CUTS,)),
+            dma((2, LINE, CUTS)),
             dma((2, LINE - 1)),
             dma((2, LINE - 1)),
             dma((2, LINE - 1, CUTS)),
@@ -443,7 +459,7 @@
             dma((3, LINE)),
         ],
         compiler_params=pltpu.CompilerParams(
-            collective_id=0, has_side_effects=True, vmem_limit_bytes=60 * 1024 * 1024
+            collective_id=0, has_side_effects=True, vmem_limit_bytes=46 * 1024 * 1024
         ),
     )(out_grad, expert_of.reshape(1, count), pre_act, down_weight[0])
     return pre_grad, summed.reshape(1, block, width)

time: 117 us -> 115 us (0.983)
  Pallas kernels: 110 us -> 107 us
    pallas_call x1, Pallas kernels: 110 us -> 107 us  [fused(): pl.pallas_call(functools.partial(kernel, experts, capacity, factor), out_...]
    unnamed x4 -> x8, local copies, waits for them, and re-layouts: 6.17 us -> 6.27 us
where the time goes in v2:
time: 115 us; the launch traced here: 114 us
  Pallas kernels  107 us (93%)
  local copies, waits for them, and re-layouts  6.27 us (5%)
    pallas_call x1, Pallas kernels, fused(): pl.pallas_call(functools.partial(kernel, experts, capacity, factor), out_...  107 us
    unnamed x8, local copies, waits for them, and re-layouts  6.27 us

profile of v2, /device:TPU:0, one launch (start us, length us, event | category | flops | bytes accessed | tf_op | source)
XLA Modules:
  0.0 114.4 jit_solution(11293474382872154281)
XLA Ops:
  0.6 0.0 copy-start
  0.6 1.2 %copy-done = bf16[1,512,1024]{2,1,0:T(8,128)(2,1)S(1)} copy-done((bf16[1,512,1024]{2,1,0:T(8,128)(2,1)S(1)}, bf16[1,512,1024]{2,1,0:T(8,128)(2,1)}, u32[]{:S(2)}) %copy-start) | copy-done | bytes 1048600
  1.9 0.0 copy-start.1
  1.9 1.0 copy-done.1
  2.9 0.0 copy-start.2
  2.9 0.7 copy-done.2
  3.6 107.4 %shard_map.59 = (bf16[512,4096]{1,0:T(8,128)(2,1)S(1)}, f32[512,1024]{1,0:T(8,128)S(1)}) custom-call(bf16[256,1024]{1,0:T(8,128)(2,1)S(1)} %copy-done.1, s32[1,256]{1,0:T(1,128)S(1)} %bitcast.5, bf16[512,4096]{1,0:T(8,128)(2,1)} %pre_hbm.1, bf16[512,1024]{1,0:T(8,128)(2,1)S(1)} %bitcast.4), custom_call_target="tpu_custom_call" | custom-call | tf_op jit(solution)/shard_map/pallas_call | solution.py:429
  111.0 2.0 %copy.8 = bf16[512,4096]{1,0:T(8,128)(2,1)} copy(bf16[512,4096]{1,0:T(8,128)(2,1)S(1)} %get-tuple-element.8) | data formatting | bytes 8388608
  113.0 1.3 %copy.9 = f32[1,512,1024]{2,1,0:T(8,128)} copy(f32[1,512,1024]{2,1,0:T(8,128)S(1)} %bitcast.3) | data formatting | bytes 4194304
Async XLA Ops:
  0.6 1.2 %copy-start = (bf16[1,512,1024]{2,1,0:T(8,128)(2,1)S(1)}, bf16[1,512,1024]{2,1,0:T(8,128)(2,1)}, u32[]{:S(2)}) copy-start(bf16[1,512,1024]{2,1,0:T(8,128)(2,1)} %param.7) | copy-start | bytes 3145732
  1.9 1.0 copy-start.1
  2.9 0.7 copy-start.2
